TPU v7x, 256 devices: a whole 4x4x8 slice. The times are simulated.
256 devices in a mesh: gx: 8 (over y_hi, x), gy: 8 (over z), gz: 4 (over y_lo, core).
Axes of the slice: x: 4, y: 4 (y_hi: 2, y_lo: 2; y = y_hi * 2 + y_lo), z: 8, core: 2. Of those that a mesh axis runs over, the one named last changes fastest.
Arguments:
- tokens: bfloat16 [4096, 49, 512], P(('gx', 'gy', 'gz')), may hold values from -6 to 6
- cotangent: bfloat16 [4096, 49, 512], P(('gx', 'gy', 'gz')), may hold values from -6 to 6
- regions: int32 [4096, 49], P(('gx', 'gy', 'gz')), may hold values from 0 to 3
- rel_index: int32 [49, 49], replicated, may hold values from 0 to 168
- w_qkv: bfloat16 [512, 1536], replicated, may hold values from -0.25 to 0.25
- w_proj: bfloat16 [512, 512], replicated, may hold values from -0.25 to 0.25
- bias_table: float32 [169, 16], replicated, may hold values from -4 to 4
- mom_qkv: float32 [786432], P(('gx', 'gy', 'gz')), may hold values from -0.06 to 0.06
- mom_proj: float32 [262144], P(('gx', 'gy', 'gz')), may hold values from -0.06 to 0.06
- mom_table: float32 [169, 16], replicated, may hold values from -0.06 to 0.06
Outputs:
- new_mom_qkv: float32 [786432], P(('gx', 'gy', 'gz'))
- new_mom_proj: float32 [262144], P(('gx', 'gy', 'gz'))
- new_mom_table: float32 [169, 16], replicated
All inputs are finite; a program needn't handle non-finite values.
Results may differ from a plain program's by a relative error of at most 0.015.
Values sent between devices are 32-bit elements; how exact they have to be, the bound alone decides.
A program may use at most 128 MiB of HBM per device.

v0:
```python
import functools

import jax
import jax.numpy as jnp
from jax import lax
from jax.experimental import pallas as pl
from jax.experimental.pallas import tpu as pltpu
from jax.sharding import PartitionSpec as P

MESH = pl.DeviceIdType.MESH
BF = jnp.bfloat16
F32 = jnp.float32
WIN = 16
TOK = 49
SEG = 64
TP = 56
D = 512
HEAD_DIM = 32
SCALE = HEAD_DIM ** -0.5
UNITS = 2


def nt(a, b):
    return lax.dot_general(a, b, (((1,), (1,)), ((), ())), preferred_element_type=F32)


def nn(a, b):
    return jnp.dot(a, b, preferred_element_type=F32)


def iota(shape, dim):
    return lax.broadcasted_iota(jnp.int32, shape, dim)


def compute_kernel(
    tok, cot, reg, rel, wqkv, wproj, tab_t, g_out, tab_out,
    xp, cp, qkv, kvt, da, xpt, bias, mask, dk, dv, dqt, at, gb, pad, tabp, relt,
):
    low = iota((TP, 128), 1) < SEG
    pad[...] = jnp.zeros_like(pad)
    pad[0:TOK, 0:TOK] = rel[...].astype(F32)
    flipped = pad[...].T
    both = flipped[0:TP] + pltpu.roll(flipped, SEG, 1)[0:TP]
    index = both.astype(jnp.int32)
    relt[...] = both
    pad[...] = jnp.zeros_like(pad)
    pad[0:WIN, 0:TOK] = reg[...].astype(F32)
    regions = pad[0:WIN, :]
    moved = pltpu.roll(regions, SEG, 1)
    columns = pad[...].T[0:TP]
    for pair in range(WIN // 2):
        w = 2 * pair
        key = jnp.where(
            low,
            jnp.broadcast_to(columns[:, w : w + 1], (TP, 128)),
            jnp.broadcast_to(columns[:, w + 1 : w + 2], (TP, 128)),
        )
        query = jnp.where(low[0:1], regions[w : w + 1], moved[w + 1 : w + 2])
        mask[pair] = jnp.where(key == query, 0.0, -100.0).astype(F32)
    tabp[...] = jnp.zeros_like(tabp)
    tabp[:, 0:169] = tab_t[...]
    first = jnp.bitwise_and(index, 127)
    beyond = index >= 128
    real = iota((TP, 128), 0) < TOK
    for h in range(16):
        lo = jnp.broadcast_to(tabp[h : h + 1, 0:128], (TP, 128))
        hi = jnp.broadcast_to(tabp[h : h + 1, 128:256], (TP, 128))
        lo = jnp.take_along_axis(lo, first, axis=1, mode="promise_in_bounds")
        hi = jnp.take_along_axis(hi, first, axis=1, mode="promise_in_bounds")
        bias[h // 4, :, (h % 4) * 128 : (h % 4 + 1) * 128] = jnp.where(
            real, jnp.where(beyond, hi, lo), -1e30
        )
    gb[...] = jnp.zeros_like(gb)

    row = iota((256, 784), 0)
    wanted = (row % SEG) * WIN + row // SEG
    column = iota((256, 784), 1)
    eye = (iota((128, 128), 0) == iota((128, 128), 1)).astype(BF)
    rho = iota((D, D), 0)
    natural = (
        ((rho >> 7) & 1) * 256
        + ((rho >> 4) & 3) * 64
        + ((rho >> 1) & 7) * 8
        + ((rho >> 6) & 1) * 4
        + ((rho >> 8) & 1) * 2
        + (rho & 1)
    )
    order = (natural == iota((D, D), 1)).astype(F32).astype(BF)

    def project(c, carry):
        rows = pl.ds(pl.multiple_of(c * 256, 256), 256)
        pick = (wanted + 4 * c == column).astype(F32).astype(BF)
        x = nn(pick, tok[...]).astype(BF)
        xp[rows, :] = x
        y = nn(pick, cot[...]).astype(BF)
        cp[rows, :] = y
        da[rows, :] = nt(y, wproj[...]).astype(BF)
        xpt[:, rows] = nt(order, x).astype(BF)
        values = nn(x, wqkv[...]).astype(BF)
        qkv[rows, :] = values
        for b in range(8):
            kvt[b * 128 : (b + 1) * 128, rows] = nt(
                eye, values[:, 512 + b * 128 : 512 + (b + 1) * 128]
            ).astype(BF)
        return carry

    lax.fori_loop(0, 4, project, 0)

    lane = iota((SEG, 128), 1)
    heads = [(lane // HEAD_DIM == h).astype(F32).astype(BF) for h in range(4)]
    zero = jnp.zeros((SEG, 128), BF)
    half = iota((SEG, 512), 1) % 128
    left = (half < SEG).astype(F32).astype(BF)
    right = (half >= SEG).astype(F32).astype(BF)
    tail = jnp.zeros((SEG - TP, 512), F32)

    def spread(a):
        blocks = []
        for h in range(4):
            blocks.append(jnp.concatenate([a[0:SEG] * heads[h], zero], axis=1))
            blocks.append(jnp.concatenate([zero, a[SEG:] * heads[h]], axis=1))
        return jnp.concatenate(blocks, axis=0)

    def side(a):
        return jnp.concatenate([a[0:SEG], a[SEG:]], axis=1)

    def attend(g, pair):
        rows = pl.ds(pl.multiple_of(pair * 128, 128), 128)
        rows0 = pl.ds(pl.multiple_of(pair * 128, 128), SEG)
        rows1 = pl.ds(pl.multiple_of(pair * 128 + SEG, SEG), SEG)

        def cols(start):
            return pl.ds(pl.multiple_of(start + g * 128, 128), 128)

        q_wide = spread(qkv[rows, cols(0)])
        scores = nt(side(qkv[rows, cols(512)]), q_wide)[0:TP] * SCALE + bias[g]
        scores = scores + jnp.concatenate([mask[pair]] * 4, axis=1)
        e = jnp.exp(scores - jnp.max(scores, axis=0, keepdims=True))
        p = e * (1.0 / jnp.sum(e, axis=0, keepdims=True))
        probs = jnp.concatenate([p, tail], axis=0).astype(BF)
        da_wide = spread(da[rows, cols(0)])
        dp = nt(side(qkv[rows, cols(1024)]), da_wide)[0:TP]
        ds = p * (dp - jnp.sum(p * dp, axis=0, keepdims=True))
        gb[g] += ds
        dsb = jnp.concatenate([ds * SCALE, tail], axis=0).astype(BF)
        dv_pair = nn(probs, da_wide).astype(BF)
        dv[rows0, cols(0)] = dv_pair[:, 0:128]
        dv[rows1, cols(0)] = dv_pair[:, 128:256]
        dk_pair = nn(dsb, q_wide).astype(BF)
        dk[rows0, cols(0)] = dk_pair[:, 0:128]
        dk[rows1, cols(0)] = dk_pair[:, 128:256]
        p_bd = jnp.concatenate([probs * left, probs * right], axis=0)
        s_bd = jnp.concatenate([dsb * left, dsb * right], axis=0)
        a_full = nn(kvt[cols(512), rows], p_bd)
        q_full = nn(kvt[cols(0), rows], s_bd)
        for h in range(4):
            strip = pl.ds(pl.multiple_of(g * 128 + 32 * h, 32), 32)
            block = (slice(32 * h, 32 * h + 32), slice(128 * h, 128 * h + 128))
            at[strip, rows] = a_full[block].astype(BF)
            dqt[strip, rows] = q_full[block].astype(BF)

    steps = WIN // 2 // UNITS

    def attention(t, carry):
        for u in range(UNITS):
            attend(t // steps, (t % steps) * UNITS + u)
        return carry

    lax.fori_loop(0, 4 * steps, attention, 0)

    def put(lo, value):
        g_out[:, :, :, :, lo : lo + 512] = value.reshape(2, 4, 4, 16, 512)

    put(0, nt(xpt[...], dqt[...]))
    put(512, nn(xpt[...], dk[...]))
    put(1024, nn(xpt[...], dv[...]))
    put(1536, nn(nn(order, at[...]).astype(BF), cp[...]))

    total = jnp.zeros((32, 256), F32)
    entry = iota((256, 128), 0).astype(F32)
    for j in range(TOK):
        hot = (entry == jnp.broadcast_to(relt[j : j + 1, :], (256, 128))).astype(F32).astype(BF)
        line = jnp.concatenate([gb[g, j : j + 1, h * 128 : (h + 1) * 128] for g in range(4) for h in range(4)], axis=0)
        upper = line.astype(BF)
        lower = (line - upper.astype(F32)).astype(BF)
        total = total + nt(jnp.concatenate([upper, lower], axis=0), hot)
    tab_out[...] = total[0:16] + total[16:32]


def compute(tok, cot, reg, rel, wqkv, wproj, tab_t):
    vm = pl.BlockSpec(memory_space=pltpu.VMEM)
    return pl.pallas_call(
        compute_kernel,
        name="grads",
        out_shape=(
            jax.ShapeDtypeStruct((2, 4, 4, 16, 2048), F32),
            jax.ShapeDtypeStruct((16, 256), F32),
        ),
        in_specs=[vm] * 7,
        out_specs=(vm, vm),
        scratch_shapes=[
            pltpu.VMEM((1024, D), BF),
            pltpu.VMEM((1024, D), BF),
            pltpu.VMEM((1024, 3 * D), BF),
            pltpu.VMEM((1024, 1024), BF),
            pltpu.VMEM((1024, D), BF),
            pltpu.VMEM((D, 1024), BF),
            pltpu.VMEM((4, TP, 512), F32),
            pltpu.VMEM((WIN // 2, TP, 128), F32),
            pltpu.VMEM((1024, D), BF),
            pltpu.VMEM((1024, D), BF),
            pltpu.VMEM((D, 1024), BF),
            pltpu.VMEM((D, 1024), BF),
            pltpu.VMEM((4, TP, 512), F32),
            pltpu.VMEM((128, 128), F32),
            pltpu.VMEM((16, 256), F32),
            pltpu.VMEM((TP, 128), F32),
        ],
        compiler_params=pltpu.CompilerParams(vmem_limit_bytes=60 * 2**20),
    )(tok, cot, reg, rel, wqkv, wproj, tab_t)


def sum_kernel(
    scale, g, tab, mom_qkv, mom_proj, mom_tab, out_qkv, out_proj, out_tab,
    s1, ra, rb, a2, b2, ra2, rb2, zs, rz, tsend, trecv, send, recv,
):
    gx, gy, gz = lax.axis_index("gx"), lax.axis_index("gy"), lax.axis_index("gz")
    x, z, core = lax.rem(gx, 4), gy, lax.rem(gz, 2)
    y = (gx // 4) * 2 + gz // 2

    def device(x, y, z, core):
        return ((y // 2) * 4 + x, z, lax.rem(y, 2) * 2 + core)

    def xor(a, b):
        out = 0
        for bit in (1, 2, 4):
            have = lax.rem(a // bit, 2)
            out = out + bit * ((1 - have) if b & bit else have)
        return out

    partner = device(x, y, z, 1 - core)
    along_x = [(xor(x, d), device(xor(x, d), y, z, core)) for d in (1, 2, 3)]
    along_y = [(xor(y, d), device(x, xor(y, d), z, core)) for d in (1, 2, 3)]
    along_z = [(xor(z, d), device(x, y, xor(z, d), core)) for d in range(1, 8)]
    peers = [partner] + [dev for _, dev in along_x + along_y + along_z]
    barrier = pltpu.get_barrier_semaphore()
    for peer in peers:
        pl.semaphore_signal(barrier, inc=1, device_id=peer, device_id_type=MESH)
    pl.semaphore_wait(barrier, len(peers))

    used = [0]

    def copy(src, dst, dev):
        n = used[0]
        used[0] += 1
        c = pltpu.make_async_remote_copy(
            src_ref=src, dst_ref=dst, send_sem=send.at[n], recv_sem=recv.at[n],
            device_id=dev, device_id_type=MESH,
        )
        c.start()
        return c

    def wait(copies):
        for c in copies:
            c.wait()

    wait([copy(g.at[1 - core], s1, partner), copy(tab, trecv.at[0], partner)])
    for b in range(4):
        s1[b] += g[core, b]
    tsend[0] = tab[...] + trecv[0]

    copies = []
    for n, (to, dev) in enumerate(along_x):
        copies.append(copy(s1.at[:, to, :, pl.ds(0, 1024)], ra.at[n], dev))
        copies.append(copy(tsend.at[0], trecv.at[1 + n], dev))
    for n, (to, dev) in enumerate(along_y):
        copies.append(copy(s1.at[to, :, :, pl.ds(1024, 1024)], rb.at[n], dev))
    wait(copies)
    for b in range(4):
        a2[b] = s1[b, x, :, 0:1024] + ra[0, b] + ra[1, b] + ra[2, b]
        b2[b] = s1[y, b, :, 1024:2048] + rb[0, b] + rb[1, b] + rb[2, b]
    tsend[1] = tsend[0] + trecv[1] + trecv[2] + trecv[3]

    copies = []
    for n, (to, dev) in enumerate(along_y):
        copies.append(copy(a2.at[to], ra2.at[n], dev))
        copies.append(copy(tsend.at[1], trecv.at[4 + n], dev))
    for n, (to, dev) in enumerate(along_x):
        copies.append(copy(b2.at[to], rb2.at[n], dev))
    wait(copies)
    a3 = a2[y] + ra2[0] + ra2[1] + ra2[2]
    b3 = b2[x] + rb2[0] + rb2[1] + rb2[2]
    for k in range(8):
        zs[k, :, 0:1024] = a3[2 * k : 2 * k + 2]
        zs[k, :, 1024:2048] = b3[2 * k : 2 * k + 2]
    tsend[2] = tsend[1] + trecv[4] + trecv[5] + trecv[6]

    copies = []
    for n, (to, dev) in enumerate(along_z):
        copies.append(copy(zs.at[to], rz.at[n], dev))
        copies.append(copy(tsend.at[2], trecv.at[7 + n], dev))
    wait(copies)
    mine = zs[z]
    table = tsend[2]
    for n in range(7):
        mine = mine + rz[n]
        table = table + trecv[7 + n]
    for r in range(2):
        for c in range(12):
            k = r * 12 + c
            out_qkv[k : k + 1, :] = 0.9 * mom_qkv[k : k + 1, :] + mine[r : r + 1, c * 128 : (c + 1) * 128] * scale
        for c in range(4):
            k = r * 4 + c
            out_proj[k : k + 1, :] = 0.9 * mom_proj[k : k + 1, :] + mine[r : r + 1, 1536 + c * 128 : 1536 + (c + 1) * 128] * scale
    out_tab[...] = 0.9 * mom_tab[...] + table[:, 0:169] * scale


def add_up(scale, g, tab, mom_qkv, mom_proj, mom_tab):
    vm = pl.BlockSpec(memory_space=pltpu.VMEM)
    return pl.pallas_call(
        functools.partial(sum_kernel, scale),
        name="add_up",
        out_shape=(
            jax.ShapeDtypeStruct((24, 128), F32),
            jax.ShapeDtypeStruct((8, 128), F32),
            jax.ShapeDtypeStruct((16, 169), F32),
        ),
        in_specs=[vm] * 5,
        out_specs=(vm, vm, vm),
        scratch_shapes=[
            pltpu.VMEM((4, 4, 16, 2048), F32),
            pltpu.VMEM((3, 4, 16, 1024), F32),
            pltpu.VMEM((3, 4, 16, 1024), F32),
            pltpu.VMEM((4, 16, 1024), F32),
            pltpu.VMEM((4, 16, 1024), F32),
            pltpu.VMEM((3, 16, 1024), F32),
            pltpu.VMEM((3, 16, 1024), F32),
            pltpu.VMEM((8, 2, 2048), F32),
            pltpu.VMEM((7, 2, 2048), F32),
            pltpu.VMEM((3, 16, 256), F32),
            pltpu.VMEM((14, 16, 256), F32),
            pltpu.SemaphoreType.DMA((40,)),
            pltpu.SemaphoreType.DMA((40,)),
        ],
        compiler_params=pltpu.CompilerParams(
            collective_id=0, has_side_effects=True, vmem_limit_bytes=40 * 2**20
        ),
    )(g, tab, mom_qkv, mom_proj, mom_tab)


def body(tokens, cotangent, regions, rel_index, w_qkv, w_proj, bias_table, mom_qkv, mom_proj, mom_table):
    win, count, dim = tokens.shape
    devices = lax.axis_size(("gx", "gy", "gz"))
    tok = jnp.transpose(tokens, (1, 0, 2)).reshape(count * win, dim)
    cot = jnp.transpose(cotangent, (1, 0, 2)).reshape(count * win, dim)
    g, tab = compute(tok, cot, regions, rel_index, w_qkv, w_proj, bias_table.T)
    out_qkv, out_proj, out_tab = add_up(
        1.0 / (win * devices), g, tab,
        mom_qkv.reshape(24, 128), mom_proj.reshape(8, 128), mom_table.T,
    )
    return out_qkv.reshape(-1), out_proj.reshape(-1), out_tab.T


def solution(mesh):
    return jax.shard_map(
        body,
        mesh=mesh,
        in_specs=(
            P(("gx", "gy", "gz"), None, None),
            P(("gx", "gy", "gz"), None, None),
            P(("gx", "gy", "gz"), None),
            P(),
            P(),
            P(),
            P(),
            P(("gx", "gy", "gz")),
            P(("gx", "gy", "gz")),
            P(),
        ),
        out_specs=(P(("gx", "gy", "gz")), P(("gx", "gy", "gz")), P()),
        check_vma=False,
    )
```

profile of v0, /device:TPU:1, one launch (start us, length us, event | category | flops | bytes accessed | tf_op | source)
XLA Modules:
  0.0 79.0 jit_solution(7935437811412895286)
XLA Ops:
  0.6 30.2 %grads.1 = (f32[2,4,4,16,2048]{4,3,2,1,0:T(8,128)}, f32[16,256]{1,0:T(8,128)}) custom-call(bf16[784,512]{1,0:T(8,128)(2,1)} %bitcast.19, bf16[784,512]{1,0:T(8,128)(2,1)} %bitcast.20, s32[16,49]{1,0:T(8,128)} %reg.1, s32[49,49]{1,0:T(8,128)} %rel.1, bf16[512,1536]{1,0:T(8,128)(2,1)} %wqkv.1, bf16[512,512]{1,0:T(8,128)(2,1)} %wproj.1, f32[16,169]{1,0:T(8,128)} %bitcast.21), custom_call_target="tpu_custom_call" | custom-call | tf_op jit(solution)/shard_map/grads/pallas_call | solution.py:192
  30.8 0.0 copy-start
  30.8 2.2 %copy-done = f32[2,4,4,16,2048]{4,3,2,1,0:T(8,128)S(1)} copy-done((f32[2,4,4,16,2048]{4,3,2,1,0:T(8,128)S(1)}, f32[2,4,4,16,2048]{4,3,2,1,0:T(8,128)}, u32[]{:S(2)}) %copy-start) | copy-done | bytes 4194328
  33.0 0.0 copy-start.1
  33.0 0.7 copy-done.1
  33.7 0.0 copy-start.2
  33.8 0.7 copy-done.2
  34.5 0.0 copy-start.3
  34.5 0.7 copy-done.3
  35.2 0.0 copy-start.4
  35.2 0.7 copy-done.4
  35.9 41.4 %add_up.1 = (f32[24,128]{1,0:T(8,128)S(1)}, f32[8,128]{1,0:T(8,128)S(1)}, f32[16,169]{1,0:T(8,128)S(1)}) custom-call(f32[2,4,4,16,2048]{4,3,2,1,0:T(8,128)S(1)} %copy-done, f32[16,256]{1,0:T(8,128)S(1)} %copy-done.2, f32[24,128]{1,0:T(8,128)S(1)} %bitcast.16, f32[8,128]{1,0:T(8,128)S(1)} %bitcast.18, f32[16,169]{1,0:T(8,128)S(1)} %bitcast.13), custom_call_target="tpu_custom_call" | custom-call | tf_op jit(solution)/shard_map/add_up/pallas_call | solution.py:320
  77.2 0.6 copy.16
  77.8 0.6 copy.17
  78.4 0.6 copy.18
Async XLA Ops:
  30.8 2.2 %copy-start = (f32[2,4,4,16,2048]{4,3,2,1,0:T(8,128)S(1)}, f32[2,4,4,16,2048]{4,3,2,1,0:T(8,128)}, u32[]{:S(2)}) copy-start(f32[2,4,4,16,2048]{4,3,2,1,0:T(8,128)} %get-tuple-element.8.g) | copy-start | bytes 12582916
  33.0 0.7 copy-start.1
  33.7 0.7 copy-start.2
  34.5 0.7 copy-start.3
  35.2 0.7 copy-start.4
where the time goes:
time: 79.8 us; the launch traced here: 79 us
  Pallas kernels  71.6 us (90%)
  local copies, waits for them, and re-layouts  6.81 us (9%)
    pallas_call x1, Pallas kernels, add_up(): pl.pallas_call(functools.partial(sum_kernel, scale), name='add_up', out_s...  41.4 us
    pallas_call x1, Pallas kernels, compute(): pl.pallas_call(compute_kernel, name='grads', out_shape=(jax.ShapeDtypeStr...  30.2 us
    unnamed x13, local copies, waits for them, and re-layouts  6.81 us

commit v1 on v0

--- a/solution.py
+++ b/solution.py
@@ -187,39 +187,6 @@
     tab_out[...] = total[0:16] + total[16:32]
 
 
-def compute(tok, cot, reg, rel, wqkv, wproj, tab_t):
-    vm = pl.BlockSpec(memory_space=pltpu.VMEM)
-    return pl.pallas_call(
-        compute_kernel,
-        name="grads",
-        out_shape=(
-            jax.ShapeDtypeStruct((2, 4, 4, 16, 2048), F32),
-            jax.ShapeDtypeStruct((16, 256), F32),
-        ),
-        in_specs=[vm] * 7,
-        out_specs=(vm, vm),
-        scratch_shapes=[
-            pltpu.VMEM((1024, D), BF),
-            pltpu.VMEM((1024, D), BF),
-            pltpu.VMEM((1024, 3 * D), BF),
-            pltpu.VMEM((1024, 1024), BF),
-            pltpu.VMEM((1024, D), BF),
-            pltpu.VMEM((D, 1024), BF),
-            pltpu.VMEM((4, TP, 512), F32),
-            pltpu.VMEM((WIN // 2, TP, 128), F32),
-            pltpu.VMEM((1024, D), BF),
-            pltpu.VMEM((1024, D), BF),
-            pltpu.VMEM((D, 1024), BF),
-            pltpu.VMEM((D, 1024), BF),
-            pltpu.VMEM((4, TP, 512), F32),
-            pltpu.VMEM((128, 128), F32),
-            pltpu.VMEM((16, 256), F32),
-            pltpu.VMEM((TP, 128), F32),
-        ],
-        compiler_params=pltpu.CompilerParams(vmem_limit_bytes=60 * 2**20),
-    )(tok, cot, reg, rel, wqkv, wproj, tab_t)
-
-
 def sum_kernel(
     scale, g, tab, mom_qkv, mom_proj, mom_tab, out_qkv, out_proj, out_tab,
     s1, ra, rb, a2, b2, ra2, rb2, zs, rz, tsend, trecv, send, recv,
@@ -315,37 +282,73 @@
     out_tab[...] = 0.9 * mom_tab[...] + table[:, 0:169] * scale
 
 
-def add_up(scale, g, tab, mom_qkv, mom_proj, mom_tab):
+LOCAL = [
+    pltpu.VMEM((1024, D), BF),
+    pltpu.VMEM((1024, D), BF),
+    pltpu.VMEM((1024, 3 * D), BF),
+    pltpu.VMEM((1024, 1024), BF),
+    pltpu.VMEM((1024, D), BF),
+    pltpu.VMEM((D, 1024), BF),
+    pltpu.VMEM((4, TP, 512), F32),
+    pltpu.VMEM((WIN // 2, TP, 128), F32),
+    pltpu.VMEM((1024, D), BF),
+    pltpu.VMEM((1024, D), BF),
+    pltpu.VMEM((D, 1024), BF),
+    pltpu.VMEM((D, 1024), BF),
+    pltpu.VMEM((4, TP, 512), F32),
+    pltpu.VMEM((128, 128), F32),
+    pltpu.VMEM((16, 256), F32),
+    pltpu.VMEM((TP, 128), F32),
+]
+SHARED = [
+    pltpu.VMEM((4, 4, 16, 2048), F32),
+    pltpu.VMEM((3, 4, 16, 1024), F32),
+    pltpu.VMEM((3, 4, 16, 1024), F32),
+    pltpu.VMEM((4, 16, 1024), F32),
+    pltpu.VMEM((4, 16, 1024), F32),
+    pltpu.VMEM((3, 16, 1024), F32),
+    pltpu.VMEM((3, 16, 1024), F32),
+    pltpu.VMEM((8, 2, 2048), F32),
+    pltpu.VMEM((7, 2, 2048), F32),
+    pltpu.VMEM((3, 16, 256), F32),
+    pltpu.VMEM((14, 16, 256), F32),
+    pltpu.SemaphoreType.DMA((40,)),
+    pltpu.SemaphoreType.DMA((40,)),
+]
+
+
+def kernel(scale, *refs):
+    inputs, refs = refs[:7], refs[7:]
+    moms, refs = refs[:3], refs[3:]
+    outs, refs = refs[:3], refs[3:]
+    g, tab, refs = refs[0], refs[1], refs[2:]
+    local, shared = refs[: len(LOCAL)], refs[len(LOCAL) :]
+    compute_kernel(*inputs, g, tab, *local)
+    sum_kernel(scale, g, tab, *moms, *outs, *shared)
+
+
+def step(scale, *operands):
     vm = pl.BlockSpec(memory_space=pltpu.VMEM)
     return pl.pallas_call(
-        functools.partial(sum_kernel, scale),
-        name="add_up",
+        functools.partial(kernel, scale),
+        name="step",
         out_shape=(
             jax.ShapeDtypeStruct((24, 128), F32),
             jax.ShapeDtypeStruct((8, 128), F32),
             jax.ShapeDtypeStruct((16, 169), F32),
         ),
-        in_specs=[vm] * 5,
+        in_specs=[vm] * 10,
         out_specs=(vm, vm, vm),
         scratch_shapes=[
-            pltpu.VMEM((4, 4, 16, 2048), F32),
-            pltpu.VMEM((3, 4, 16, 1024), F32),
-            pltpu.VMEM((3, 4, 16, 1024), F32),
-            pltpu.VMEM((4, 16, 1024), F32),
-            pltpu.VMEM((4, 16, 1024), F32),
-            pltpu.VMEM((3, 16, 1024), F32),
-            pltpu.VMEM((3, 16, 1024), F32),
-            pltpu.VMEM((8, 2, 2048), F32),
-            pltpu.VMEM((7, 2, 2048), F32),
-            pltpu.VMEM((3, 16, 256), F32),
-            pltpu.VMEM((14, 16, 256), F32),
-            pltpu.SemaphoreType.DMA((40,)),
-            pltpu.SemaphoreType.DMA((40,)),
+            pltpu.VMEM((2, 4, 4, 16, 2048), F32),
+            pltpu.VMEM((16, 256), F32),
+            *LOCAL,
+            *SHARED,
         ],
         compiler_params=pltpu.CompilerParams(
-            collective_id=0, has_side_effects=True, vmem_limit_bytes=40 * 2**20
+            collective_id=0, has_side_effects=True, vmem_limit_bytes=60 * 2**20
         ),
-    )(g, tab, mom_qkv, mom_proj, mom_tab)
+    )(*operands)
 
 
 def body(tokens, cotangent, regions, rel_index, w_qkv, w_proj, bias_table, mom_qkv, mom_proj, mom_table):
@@ -353,9 +356,8 @@
     devices = lax.axis_size(("gx", "gy", "gz"))
     tok = jnp.transpose(tokens, (1, 0, 2)).reshape(count * win, dim)
     cot = jnp.transpose(cotangent, (1, 0, 2)).reshape(count * win, dim)
-    g, tab = compute(tok, cot, regions, rel_index, w_qkv, w_proj, bias_table.T)
-    out_qkv, out_proj, out_tab = add_up(
-        1.0 / (win * devices), g, tab,
+    out_qkv, out_proj, out_tab = step(
+        1.0 / (win * devices), tok, cot, regions, rel_index, w_qkv, w_proj, bias_table.T,
         mom_qkv.reshape(24, 128), mom_proj.reshape(8, 128), mom_table.T,
     )
     return out_qkv.reshape(-1), out_proj.reshape(-1), out_tab.T

time: 79.8 us -> 76.8 us (0.962)
  local copies, waits for them, and re-layouts: 6.81 us -> 3.9 us
    unnamed x13 -> x3, local copies, waits for them, and re-layouts: 6.81 us -> 3.9 us
    pallas_call x2 -> x1, Pallas kernels: 71.6 us -> 71.6 us  [step(): pl.pallas_call(functools.partial(kernel, scale), name='step', out_shape=(...]
where the time goes in v1:
time: 76.8 us; the launch traced here: 76.1 us
  Pallas kernels  71.6 us (93%)
  local copies, waits for them, and re-layouts  3.9 us (5%)
    pallas_call x1, Pallas kernels, step(): pl.pallas_call(functools.partial(kernel, scale), name='step', out_shape=(...  71.6 us
    unnamed x3, local copies, waits for them, and re-layouts  3.9 us

profile of v1, /device:TPU:1, one launch (start us, length us, event | category | flops | bytes accessed | tf_op | source)
XLA Modules:
  0.0 76.1 jit_solution(11353101646710489629)
XLA Ops:
  0.6 71.6 %step.1 = (f32[24,128]{1,0:T(8,128)}, f32[8,128]{1,0:T(8,128)}, f32[16,169]{1,0:T(8,128)}) custom-call(bf16[784,512]{1,0:T(8,128)(2,1)} %bitcast.13, bf16[784,512]{1,0:T(8,128)(2,1)} %bitcast.14, s32[16,49]{1,0:T(8,128)} %refs_2_.1, s32[49,49]{1,0:T(8,128)} %refs_3_.1, bf16[512,1536]{1,0:T(8,128)(2,1)} %refs_4_.1, bf16[512,512]{1,0:T(8,128)(2,1)} %refs_5_.1, ...), custom_call_target="tpu_custom_call" | custom-call | tf_op jit(solution)/shard_map/step/pallas_call | solution.py:332
  72.2 1.3 %copy.16 = f32[3072]{0:T(1024)} copy(f32[3072]{0:T(1024)} %bitcast.18) | data formatting | bytes 24576
  73.5 1.3 %copy.17 = f32[1024]{0:T(1024)} copy(f32[1024]{0:T(1024)} %bitcast.21) | data formatting | bytes 8192
  74.8 1.3 %copy.18 = f32[169,16]{0,1:T(8,128)} copy(f32[169,16]{0,1:T(8,128)} %bitcast.17) | data formatting | bytes 21632
